TPU v7x, 32 devices: a whole 2x2x4 slice. The times are simulated.
32 devices in a mesh: dp: 8 (over y, x, core), sp: 4 (over z).
Axes of the slice: x: 2, y: 2, z: 4, core: 2. Of those that a mesh axis runs over, the one named last changes fastest.
Arguments:
- queries: bfloat16 [4096, 8192], P(('dp', 'sp')), may hold values from -17.5 to 17.5
- key_rows: bfloat16 [4096, 1024], P(('dp', 'sp')), may hold values from -3.5 to 3.5
- value_rows: bfloat16 [4096, 1024], P(('dp', 'sp')), may hold values from -6 to 6
- grad_out: bfloat16 [4096, 8192], P(('dp', 'sp')), may hold values from -6 to 6
- doc_ids: int32 [4096], P(('dp', 'sp')), may hold values from 0 to 15, never falling along the last dimension, each value on 1 to 512 neighbouring positions
Outputs:
- attended: bfloat16 [4096, 8192], P(('dp', 'sp'))
- grad_queries: bfloat16 [4096, 8192], P(('dp', 'sp'))
- grad_keys: bfloat16 [4096, 1024], P(('dp', 'sp'))
- grad_values: bfloat16 [4096, 1024], P(('dp', 'sp'))
Inputs may be any that keep to these rules, and one draw needn't show every extreme that they name: `doc_ids`: document numbers never fall along the tokens; every document has 1 to 512 tokens and one has exactly 512.
All inputs are finite; a program needn't handle non-finite values.
Results may differ from a plain program's by a relative error of at most 0.011.
Values may be sent and summed in bfloat16 or wider, within the bound.
A program may use at most 128 MiB of HBM per device.

v0:
```python
import jax
import jax.numpy as jnp
from jax import lax
from jax.sharding import PartitionSpec as P

DH = 128


NEGATIVE = -1e30


def from_behind(block, axis, distance):
    devices = range(lax.axis_size(axis))
    route = [(i - distance, i) for i in devices if i - distance in devices]
    return lax.ppermute(block, axis, route)


def band_mask(query_docs, query_pos, key_docs, key_pos):
    same = query_docs[:, None] == key_docs[None, :]
    return same & (key_pos[None, :] <= query_pos[:, None]) & (key_pos[None, :] >= 0)


def group_probs(query_group, key_group, mask):
    scores = jnp.einsum(
        "qhd,wd->hqw", query_group, key_group, preferred_element_type=jnp.float32
    ) * DH ** (-0.5)
    scores = jnp.where(mask[None], scores, NEGATIVE)
    expo = jnp.exp(scores - jnp.max(scores, axis=-1, keepdims=True))
    return expo / jnp.sum(expo, axis=-1, keepdims=True)


def group_attend(items, mask):
    query_group, key_group, value_group = items
    weights = group_probs(query_group, key_group, mask).astype(jnp.bfloat16)
    return jnp.einsum(
        "hqw,wd->qhd", weights, value_group, preferred_element_type=jnp.float32
    ).astype(jnp.bfloat16)


def group_grads(items, mask):
    query_group, key_group, value_group, grad_group, output_group = items
    probs = group_probs(query_group, key_group, mask)
    weights = probs.astype(jnp.bfloat16)
    dprobs = jnp.einsum("qhd,wd->hqw", grad_group, value_group, preferred_element_type=jnp.float32)
    delta = jnp.sum(grad_group.astype(jnp.float32) * output_group.astype(jnp.float32), axis=-1).T
    dscores = (probs * (dprobs - delta[:, :, None]) * DH ** (-0.5)).astype(jnp.bfloat16)
    grad_query = jnp.einsum(
        "hqw,wd->qhd", dscores, key_group, preferred_element_type=jnp.float32
    ).astype(jnp.bfloat16)
    grad_key = jnp.einsum("hqw,qhd->wd", dscores, query_group, preferred_element_type=jnp.float32)
    grad_value = jnp.einsum("hqw,qhd->wd", weights, grad_group, preferred_element_type=jnp.float32)
    return (grad_query, grad_key, grad_value)


def split_heads(rows, groups):
    return rows.reshape(rows.shape[0], groups, -1, DH).transpose(1, 0, 2, 3)


def split_keys(rows, groups):
    return rows.reshape(rows.shape[0], groups, DH).transpose(1, 0, 2)


def block_inputs(
    query_rows, key_cat, value_cat, query_docs, query_pos, key_docs, key_pos, offset, start, width
):
    groups = key_cat.shape[1] // DH
    window = offset + start
    mask = band_mask(
        query_docs,
        query_pos,
        lax.dynamic_slice_in_dim(key_docs, window, width, 0),
        lax.dynamic_slice_in_dim(key_pos, window, width, 0),
    )
    query_block = split_heads(query_rows, groups)
    key_window = split_keys(lax.dynamic_slice_in_dim(key_cat, window, width, 0), groups)
    value_window = split_keys(lax.dynamic_slice_in_dim(value_cat, window, width, 0), groups)
    return (mask, query_block, key_window, value_window, window, groups)


def run_forward(query_rows, key_cat, value_cat, query_docs, query_pos, key_docs, key_pos, offset):
    rows = query_rows.shape[0]
    block_rows = min(512, rows)
    width = key_cat.shape[0] // 2 + block_rows

    def advance(step, buffer):
        start = step * block_rows
        mask, query_block, key_window, value_window, window, groups = block_inputs(
            query_rows,
            key_cat,
            value_cat,
            query_docs,
            query_pos,
            key_docs,
            key_pos,
            offset,
            start,
            width,
        )
        outputs = lax.map(
            lambda items: group_attend(items, mask), (query_block, key_window, value_window)
        )
        merged = outputs.transpose(1, 0, 2, 3).reshape(block_rows, -1)
        return merged

    return lax.fori_loop(0, rows // block_rows, advance, jnp.zeros(query_rows.shape, jnp.bfloat16))


def run_backward(
    query_rows,
    key_cat,
    value_cat,
    grad_rows,
    output_rows,
    query_docs,
    query_pos,
    key_docs,
    key_pos,
    offset,
):
    rows = query_rows.shape[0]
    block_rows = min(512, rows)
    width = key_cat.shape[0] // 2 + block_rows

    def advance(step, carry):
        query_grads, key_acc, value_acc = carry
        start = step * block_rows
        mask, query_block, key_window, value_window, window, groups = block_inputs(
            query_rows,
            key_cat,
            value_cat,
            query_docs,
            query_pos,
            key_docs,
            key_pos,
            offset,
            start,
            width,
        )
        grad_block = split_heads(grad_rows, groups)
        output_block = split_heads(output_rows, groups)
        grad_qs, grad_ks, grad_vs = lax.map(
            lambda items: group_grads(items, mask),
            (query_block, key_window, value_window, grad_block, output_block),
        )
        query_grads = grad_qs.transpose(1, 0, 2, 3).reshape(block_rows, -1)
        key_part = grad_ks.transpose(1, 0, 2).reshape(width, -1)
        value_part = grad_vs.transpose(1, 0, 2).reshape(width, -1)
        key_acc = lax.dynamic_update_slice_in_dim(
            key_acc, lax.dynamic_slice_in_dim(key_acc, window, width, 0) + key_part, window, 0
        )
        value_acc = lax.dynamic_update_slice_in_dim(
            value_acc, lax.dynamic_slice_in_dim(value_acc, window, width, 0) + value_part, window, 0
        )
        return (query_grads, key_acc, value_acc)

    zeros = jnp.zeros(key_cat.shape, jnp.float32)
    start_carry = (jnp.zeros(query_rows.shape, jnp.bfloat16), zeros, zeros)
    return lax.fori_loop(0, rows // block_rows, advance, start_carry)


def shards(queries, key_rows, value_rows, grad_out, doc_ids):
    dev_rows = queries.shape[0]
    row_len = dev_rows * lax.axis_size("sp")
    row_index = lax.axis_index("dp")
    col_index = lax.axis_index("sp")
    row_docs = lax.all_gather(doc_ids, "sp", axis=0, tiled=True)
    prior_docs = from_behind(row_docs, "dp", 1)
    key_docs = jnp.concatenate([prior_docs, row_docs], axis=0)
    key_pos = (row_index - 1) * row_len + jnp.arange(2 * row_len, dtype=jnp.int32)
    whole_keys, whole_values = (
        lax.all_gather(key_rows, "sp", axis=0, tiled=True),
        lax.all_gather(value_rows, "sp", axis=0, tiled=True),
    )
    prior_keys, prior_values = from_behind((whole_keys, whole_values), "dp", 1)
    key_cat = jnp.concatenate([prior_keys, whole_keys], axis=0)
    value_cat = jnp.concatenate([prior_values, whole_values], axis=0)
    offset = col_index * dev_rows
    query_pos = row_index * row_len + offset + jnp.arange(dev_rows, dtype=jnp.int32)
    attended = run_forward(
        queries, key_cat, value_cat, doc_ids, query_pos, key_docs, key_pos, offset
    )
    grad_queries, key_acc, value_acc = run_backward(
        queries,
        key_cat,
        value_cat,
        grad_out,
        attended,
        doc_ids,
        query_pos,
        key_docs,
        key_pos,
        offset,
    )
    later_keys, later_values = (
        from_behind(key_acc[:row_len].astype(jnp.bfloat16), "dp", -1).astype(jnp.float32),
        from_behind(value_acc[:row_len].astype(jnp.bfloat16), "dp", -1).astype(jnp.float32),
    )
    summed_keys, summed_values = (
        lax.psum_scatter(key_acc[row_len:] + later_keys, "sp", scatter_dimension=0, tiled=True),
        lax.psum_scatter(value_acc[row_len:] + later_values, "sp", scatter_dimension=0, tiled=True),
    )
    grad_keys = summed_keys.astype(jnp.bfloat16)
    grad_values = summed_values.astype(jnp.bfloat16)
    return (attended, grad_queries, grad_keys, grad_values)


def solution(mesh):
    placed = (
        P(("dp", "sp"), None),
        P(("dp", "sp"), None),
        P(("dp", "sp"), None),
        P(("dp", "sp"), None),
        P(("dp", "sp")),
    )
    return jax.shard_map(
        shards,
        mesh=mesh,
        in_specs=placed,
        out_specs=(
            P(("dp", "sp"), None),
            P(("dp", "sp"), None),
            P(("dp", "sp"), None),
            P(("dp", "sp"), None),
        ),
        check_vma=False,
    )
```

profile of v0, /device:TPU:0, one launch (start us, length us, event | category | flops | bytes accessed | tf_op | source)
XLA Modules:
  0.0 380.9 jit_solution(5255218137836279076)
XLA Ops:
  10.9 31.9 %all-gather.6.cloned.1.call-done = bf16[512,1024]{0,1:T(8,128)(2,1)} async-done(((bf16[128,1024]{0,1:T(8,128)(2,1)}), bf16[512,1024]{0,1:T(8,128)(2,1)}) %all-gather.6.cloned.1.call-update) | async-done | bytes 1048592 | tf_op jit(solution)/shard_map/all_gather | solution.py:171
  45.1 28.1 %all-gather.4.cloned.1.call-done = bf16[512,1024]{0,1:T(8,128)(2,1)} async-done(((bf16[128,1024]{0,1:T(8,128)(2,1)}), bf16[512,1024]{0,1:T(8,128)(2,1)}) %all-gather.4.cloned.1.call-update) | async-done | bytes 1048592 | tf_op jit(solution)/shard_map/all_gather | solution.py:172
  75.5 10.2 %all-gather = s32[4,1,128]{2,1,0:T(1,128)S(1)} all-gather(s32[1,1,128]{2,1,0:T(1,128)} %bitcast.230), channel_id=1, replica_groups=mesh['dp'=8,'sp'=4] {'sp'}, dimensions={0}, use_global_device_ids=true | all-gather | bytes 2560 | tf_op jit(solution)/shard_map/all_gather | solution.py:166
  87.1 3.2 copy.41
  92.9 4.2 %copy.45 = bf16[128,8192]{0,1:T(8,128)(2,1)} copy(bf16[128,8192]{1,0:T(8,128)(2,1)} %param.12) | data formatting | bytes 4194304 | tf_op args[3]
  99.7 2.7 fusion.123
  102.9 37.4 %while.46 = (s32[]{:T(128)}, bf16[8,128,8,128]{1,3,2,0:T(8,128)(2,1)S(1)}, bf16[8,640,128]{1,2,0:T(8,128)(2,1)}, bf16[8,640,128]{2,1,0:T(8,128)(2,1)S(1)}, bf16[...) while((s32[]{:T(128)}, ...), condition=%wide.region_3.4_spmd.clone, body=%wide.region_0.3_spmd.clone.sunk | while | flops 509675776 | bytes 1541869 | solution.py:99
  142.1 123.9 %while.47 = (s32[]{:T(128)}, bf16[8,128,8,128]{1,3,2,0:T(8,128)(2,1)}, f32[8,640,128]{2,1,0:T(8,128)}, f32[8,640,128]{2,1,0:T(8,128)}, bf16[8,640,128]{2,1,0:T(8...) while((s32[]{:T(128)}, ...), condition=%wide.region_8.9_spmd.clone, body=%wide.region_4.0_spmd.clone.sunk | while | flops 1016792320 | bytes 25445192 | solution.py:141
  145.1 3.5 fusion.183
  154.5 3.1 fusion.187
  160.6 3.5 fusion.183
  170.0 3.1 fusion.187
  176.1 3.5 fusion.183
  179.6 2.6 fusion.184
  185.5 3.1 fusion.187
  191.6 3.5 fusion.183
  201.0 3.1 fusion.187
  207.1 3.5 fusion.183
  216.5 3.1 fusion.187
  222.6 3.5 fusion.183
  232.0 3.1 fusion.187
  238.0 3.5 fusion.183
  241.5 2.6 fusion.184
  247.5 3.1 fusion.187
  253.5 3.5 fusion.183
  263.0 3.1 fusion.187
  269.6 3.3 collective-permute-done.4
  278.1 14.0 %collective-permute-done.3 = bf16[512,1024]{1,0:T(8,128)(2,1)S(1)} collective-permute-done((bf16[512,1024]{1,0:T(8,128)(2,1)S(1)}, bf16[512,1024]{1,0:T(8,128)(2,1)S(1)}, u32[]{:S(2)}, u32[]{:S(2)}) %collective-permute-start.3) | collective-permute-done | bytes 1048608 | tf_op jit(solution)/shard_map/ppermute | solution.py:15
  293.7 4.1 %copy.58 = bf16[128,8192]{1,0:T(8,128)(2,1)} copy(bf16[128,8192]{0,1:T(8,128)(2,1)} %bitcast.224) | data formatting | bytes 4194304 | tf_op jit(solution)/shard_map/while/body/eval_jaxpr/reshape | solution.py:145
  297.8 2.9 copy.57
  300.7 26.9 %reduce-scatter.5.cloned.1.call-done = f32[128,1024]{1,0:T(8,128)} async-done(((f32[512,1024]{1,0:T(8,128)}), f32[128,1024]{1,0:T(8,128)}) %reduce-scatter.5.cloned.1.call-update) | async-done | bytes 524304 | tf_op jit(solution)/shard_map/reduce_scatter | solution.py:200
  329.3 43.3 %reduce-scatter.3.cloned.1.call-done = f32[128,1024]{1,0:T(8,128)} async-done(((f32[512,1024]{1,0:T(8,128)}), f32[128,1024]{1,0:T(8,128)}) %reduce-scatter.3.cloned.1.call-update) | async-done | bytes 524304 | tf_op jit(solution)/shard_map/reduce_scatter | solution.py:199
  (166 shorter events, 133.9 us)
Async XLA Ops:
  7.2 35.6 %all-gather.6.cloned.1.call-start = ((), (), s32[]{:S(2)}) async-start(), calls=%async_computation.3 | async-start | bytes 1310720 | tf_op jit(solution)/shard_map/all_gather | solution.py:171
  9.0 64.2 %all-gather.4.cloned.1.call-start = ((), (), s32[]{:S(2)}) async-start(), calls=%async_computation.2 | async-start | bytes 1310720 | tf_op jit(solution)/shard_map/all_gather | solution.py:172
  10.9 316.6 %reduce-scatter.5.cloned.1.call-start = ((), (), s32[]{:S(2)}) async-start(), calls=%async_computation.5 | async-start | bytes 2621440 | tf_op jit(solution)/shard_map/reduce_scatter | solution.py:200
  42.8 54.4 %collective-permute-start.2 = (bf16[512,1024]{0,1:T(8,128)(2,1)}, bf16[512,1024]{0,1:T(8,128)(2,1)}, u32[]{:S(2)}, u32[]{:S(2)}) collective-permute-start(bf16[512,1024]{0,1:T(8,128)(2,1)} %all-gather.6.cloned.1.call-done), channel_id=1, source_target_pairs={{0,4},{4,8},{8,12},{12,16},{16,20},{20,24},{24,28},{1,5},{5,9},{9,... | collective-permute-start | bytes 3145736 | tf_op jit(solution)/shard_map/ppermute | solution.py:15
  73.2 26.5 %collective-permute-start = (bf16[512,1024]{0,1:T(8,128)(2,1)}, bf16[512,1024]{0,1:T(8,128)(2,1)}, u32[]{:S(2)}, u32[]{:S(2)}) collective-permute-start(bf16[512,1024]{0,1:T(8,128)(2,1)} %all-gather.4.cloned.1.call-done), channel_id=1, source_target_pairs={{0,4},{4,8},{8,12},{12,16},{16,20},{20,24},{24,28},{1,5},{5,9},{9,... | collective-permute-start | bytes 3145736 | tf_op jit(solution)/shard_map/ppermute | solution.py:15
  85.7 11.4 %collective-permute-start.1 = (s32[512]{0:T(512)S(1)}, s32[512]{0:T(512)S(1)}, u32[]{:S(2)}, u32[]{:S(2)}) collective-permute-start(s32[512]{0:T(512)S(1)} %bitcast.231), channel_id=1, source_target_pairs={{0,4},{4,8},{8,12},{12,16},{16,20},{20,24},{24,28},{1,5},{5,9},{9,... | collective-permute-start | bytes 6152 | tf_op jit(solution)/shard_map/ppermute | solution.py:15
  92.9 4.2 %copy-start.4 = (bf16[512,1024]{0,1:T(8,128)(2,1)S(1)}, bf16[512,1024]{0,1:T(8,128)(2,1)}, u32[]{:S(2)}) copy-start(bf16[512,1024]{0,1:T(8,128)(2,1)} %all-gather.6.cloned.1.call-done) | copy-start | bytes 3145732
  99.7 3.3 copy-start.5
  142.1 1.1 copy-start
  148.6 4.8 %copy-start.1 = (bf16[8,640,128]{2,1,0:T(8,128)(2,1)S(1)}, bf16[8,640,128]{2,1,0:T(8,128)(2,1)}, u32[]{:S(2)}) copy-start(bf16[8,640,128]{2,1,0:T(8,128)(2,1)} %copy-done) | copy-start | bytes 3932164 | tf_op jit(solution)/shard_map/while/body/eval_jaxpr/while
  157.6 1.1 copy-start
  164.1 4.8 %copy-start.1 = (bf16[8,640,128]{2,1,0:T(8,128)(2,1)S(1)}, bf16[8,640,128]{2,1,0:T(8,128)(2,1)}, u32[]{:S(2)}) copy-start(bf16[8,640,128]{2,1,0:T(8,128)(2,1)} %copy-done) | copy-start | bytes 3932164 | tf_op jit(solution)/shard_map/while/body/eval_jaxpr/while
  173.1 1.1 copy-start
  179.6 4.8 %copy-start.1 = (bf16[8,640,128]{2,1,0:T(8,128)(2,1)S(1)}, bf16[8,640,128]{2,1,0:T(8,128)(2,1)}, u32[]{:S(2)}) copy-start(bf16[8,640,128]{2,1,0:T(8,128)(2,1)} %copy-done) | copy-start | bytes 3932164 | tf_op jit(solution)/shard_map/while/body/eval_jaxpr/while
  188.6 1.1 copy-start
  195.1 4.8 %copy-start.1 = (bf16[8,640,128]{2,1,0:T(8,128)(2,1)S(1)}, bf16[8,640,128]{2,1,0:T(8,128)(2,1)}, u32[]{:S(2)}) copy-start(bf16[8,640,128]{2,1,0:T(8,128)(2,1)} %copy-done) | copy-start | bytes 3932164 | tf_op jit(solution)/shard_map/while/body/eval_jaxpr/while
  204.1 1.1 copy-start
  210.6 4.8 %copy-start.1 = (bf16[8,640,128]{2,1,0:T(8,128)(2,1)S(1)}, bf16[8,640,128]{2,1,0:T(8,128)(2,1)}, u32[]{:S(2)}) copy-start(bf16[8,640,128]{2,1,0:T(8,128)(2,1)} %copy-done) | copy-start | bytes 3932164 | tf_op jit(solution)/shard_map/while/body/eval_jaxpr/while
  219.6 1.1 copy-start
  226.1 4.8 %copy-start.1 = (bf16[8,640,128]{2,1,0:T(8,128)(2,1)S(1)}, bf16[8,640,128]{2,1,0:T(8,128)(2,1)}, u32[]{:S(2)}) copy-start(bf16[8,640,128]{2,1,0:T(8,128)(2,1)} %copy-done) | copy-start | bytes 3932164 | tf_op jit(solution)/shard_map/while/body/eval_jaxpr/while
  235.1 1.1 copy-start
  241.5 4.8 %copy-start.1 = (bf16[8,640,128]{2,1,0:T(8,128)(2,1)S(1)}, bf16[8,640,128]{2,1,0:T(8,128)(2,1)}, u32[]{:S(2)}) copy-start(bf16[8,640,128]{2,1,0:T(8,128)(2,1)} %copy-done) | copy-start | bytes 3932164 | tf_op jit(solution)/shard_map/while/body/eval_jaxpr/while
  250.6 1.1 copy-start
  257.0 4.8 %copy-start.1 = (bf16[8,640,128]{2,1,0:T(8,128)(2,1)S(1)}, bf16[8,640,128]{2,1,0:T(8,128)(2,1)}, u32[]{:S(2)}) copy-start(bf16[8,640,128]{2,1,0:T(8,128)(2,1)} %copy-done) | copy-start | bytes 3932164 | tf_op jit(solution)/shard_map/while/body/eval_jaxpr/while
  266.1 1.7 copy-start.3
  268.3 4.6 %collective-permute-start.4 = (bf16[512,1024]{1,0:T(8,128)(2,1)S(1)}, bf16[512,1024]{1,0:T(8,128)(2,1)S(1)}, u32[]{:S(2)}, u32[]{:S(2)}) collective-permute-start(bf16[512,1024]{1,0:T(8,128)(2,1)S(1)} %slice.26), channel_id=1, source_target_pairs={{4,0},{8,4},{12,8},{16,12},{20,16},{24,20},{28,24},{5,1},{9,5},{13... | collective-permute-start | bytes 3145736 | tf_op jit(solution)/shard_map/ppermute | solution.py:15
  274.5 98.1 %reduce-scatter.3.cloned.1.call-start = ((), (), s32[]{:S(2)}) async-start(), calls=%async_computation.4 | async-start | bytes 2621440 | tf_op jit(solution)/shard_map/reduce_scatter | solution.py:199
  274.6 1.7 copy-start.2
  276.8 15.3 %collective-permute-start.3 = (bf16[512,1024]{1,0:T(8,128)(2,1)S(1)}, bf16[512,1024]{1,0:T(8,128)(2,1)S(1)}, u32[]{:S(2)}, u32[]{:S(2)}) collective-permute-start(bf16[512,1024]{1,0:T(8,128)(2,1)S(1)} %slice.27), channel_id=1, source_target_pairs={{4,0},{8,4},{12,8},{16,12},{20,16},{24,20},{28,24},{5,1},{9,5},{13... | collective-permute-start | bytes 3145736 | tf_op jit(solution)/shard_map/ppermute | solution.py:15
Sparse Core Ops, SparseCore 0:
  10.1 32.6 all-gather.5
  44.9 28.2 all-gather.3
  274.6 52.8 reduce-scatter.4
  329.7 42.8 reduce-scatter.2
where the time goes:
time: 383 us; the launch traced here: 381 us
  waiting for transfers between devices  147 us (38%)
  matrix products  135 us (35%)
  local copies, waits for them, and re-layouts  47.4 us (12%)
  other arithmetic  18.1 us (5%)
  between operations  13.9 us (4%)
  blocking collectives  10.2 us (3%)
  starting transfers between devices  8.57 us (2%)
    sub x16, matrix products, group_probs(): expo = jnp.exp(scores - jnp.max(scores, axis=-1, keepdims=True))  43.5 us
    reduce_scatter x1, waiting for transfers between devices, shards(): lax.psum_scatter(key_acc[row_len:] + later_keys, 'sp', scatter_dimension=...  43.3 us
    all_gather x1, waiting for transfers between devices, shards(): lax.all_gather(key_rows, 'sp', axis=0, tiled=True)  31.9 us
    all_gather x1, waiting for transfers between devices, shards(): lax.all_gather(value_rows, 'sp', axis=0, tiled=True)  28.1 us
    reduce_scatter x1, waiting for transfers between devices, shards(): lax.psum_scatter(value_acc[row_len:] + later_values, 'sp', scatter_dimens...  26.9 us
    dot_general x8, matrix products, group_grads(): jnp.einsum('hqw,qhd->wd', weights, grad_group, preferred_element_type=jnp...  24.7 us
    dot_general x8, matrix products, group_grads(): jnp.einsum('qhd,wd->hqw', grad_group, value_group, preferred_element_type...  20.9 us
    dot_general x8, matrix products, group_attend(): jnp.einsum('hqw,wd->qhd', weights, value_group, preferred_element_type=jn...  19.1 us
  transfers between devices with their start and end apart: 9, of which 6 were waited for; matrix products, arithmetic and copies ran while one was open for 7% of the time, Pallas kernels for 0%

commit v1 on v0

v1 whole, which is shorter than its diff:
```python
import functools
import math

import jax
import jax.numpy as jnp
from jax import lax
from jax.experimental import pallas as pl
from jax.experimental.pallas import tpu as pltpu
from jax.sharding import PartitionSpec as P

DH = 128
NEGATIVE = -1e30
MESH = pl.DeviceIdType.MESH
PAIR = 2


def kernel(
    ndp, nsp, groups, heads,
    q_hbm, k_hbm, v_hbm, g_hbm, ids_hbm,
    att_hbm, gq_hbm, gk_hbm, gv_hbm,
    q_buf, g_buf, att_buf, gq_buf, kv_buf, ids_buf, bias, pt_buf, ds_buf,
    part_own, part_send, part_recv, gk_buf, gv_buf,
    load_sem, out_sem, kv_load, kv_send, kv_recv, ids_send, ids_recv, ids_load,
    pg_send, pg_recv, fin_sem,
):
    me = lax.axis_index("dp") * nsp + lax.axis_index("sp")
    total = ndp * nsp
    blocks = nsp + 1
    rows = q_hbm.shape[0]
    scale = DH ** (-0.5)

    def device(index):
        return (index // nsp, lax.rem(index, nsp))

    def head_cols(g):
        return pl.ds(pl.multiple_of(g * (heads * DH), heads * DH), heads * DH)

    def key_cols(g):
        return pl.ds(pl.multiple_of(g * DH, DH), DH)

    def load_k(g):
        return pltpu.make_async_copy(k_hbm.at[:, key_cols(g)], kv_buf.at[g, nsp, 0], kv_load.at[g, 0])

    def load_v(g):
        return pltpu.make_async_copy(v_hbm.at[:, key_cols(g)], kv_buf.at[g, nsp, 1], kv_load.at[g, 1])

    def load_q(g):
        return pltpu.make_async_copy(q_hbm.at[:, head_cols(g)], q_buf.at[g], load_sem.at[g, 0])

    def load_g(g):
        return pltpu.make_async_copy(g_hbm.at[:, head_cols(g)], g_buf.at[g], load_sem.at[g, 1])

    def store_att(g):
        return pltpu.make_async_copy(att_buf.at[g], att_hbm.at[:, head_cols(g)], out_sem.at[g, 0])

    def store_gq(g):
        return pltpu.make_async_copy(gq_buf.at[g], gq_hbm.at[:, head_cols(g)], out_sem.at[g, 1])

    def send_kv(g, dist):
        return pltpu.make_async_remote_copy(
            src_ref=kv_buf.at[g, nsp], dst_ref=kv_buf.at[g, nsp - dist],
            send_sem=kv_send.at[g, dist - 1], recv_sem=kv_recv.at[g, dist - 1],
            device_id=device(me + dist), device_id_type=MESH)

    def send_ids(dist):
        return pltpu.make_async_remote_copy(
            src_ref=ids_buf.at[nsp], dst_ref=ids_buf.at[nsp - dist],
            send_sem=ids_send.at[dist - 1], recv_sem=ids_recv.at[dist - 1],
            device_id=device(me + dist), device_id_type=MESH)

    def send_part(g, dist):
        return pltpu.make_async_remote_copy(
            src_ref=part_send.at[g, dist - 1], dst_ref=part_recv.at[g, dist - 1],
            send_sem=pg_send.at[g, dist - 1], recv_sem=pg_recv.at[g, dist - 1],
            device_id=device(me - dist), device_id_type=MESH)

    ids_copy = pltpu.make_async_copy(ids_hbm, ids_buf.at[nsp], ids_load)
    ids_copy.start()
    for g in range(groups):
        load_k(g).start()
        load_v(g).start()
    for g in range(groups):
        load_q(g).start()
        load_g(g).start()

    barrier = pltpu.get_barrier_semaphore()
    for dist in range(1, nsp + 1):
        @pl.when(me + dist < total)
        def _():
            pl.semaphore_signal(barrier, inc=1, device_id=device(me + dist), device_id_type=MESH)

        @pl.when(me - dist >= 0)
        def _():
            pl.semaphore_signal(barrier, inc=1, device_id=device(me - dist), device_id_type=MESH)

    peers = jnp.minimum(nsp, total - 1 - me) + jnp.minimum(nsp, me)
    pl.semaphore_wait(barrier, peers)

    ids_copy.wait()
    for dist in range(1, nsp + 1):
        @pl.when(me + dist < total)
        def _():
            send_ids(dist).start()

    def start_kv(g, carry):
        load_k(g).wait()
        load_v(g).wait()
        for dist in range(1, nsp + 1):
            @pl.when(me + dist < total)
            def _():
                send_kv(g, dist).start()
        return carry

    lax.fori_loop(0, groups, start_kv, 0)

    for dist in range(1, nsp + 1):
        @pl.when(me - dist < 0)
        def _():
            ids_buf[nsp - dist] = jnp.full((8, rows), -1.0, jnp.float32)

            def clear(g, carry):
                kv_buf[g, nsp - dist] = jnp.zeros((2, rows, DH), jnp.bfloat16)
                return carry

            lax.fori_loop(0, groups, clear, 0)

        @pl.when(me - dist >= 0)
        def _():
            send_ids(dist).wait_recv()

    own = jnp.broadcast_to(ids_buf[nsp][0:1], (rows, rows))
    for slot in range(blocks):
        other = jnp.broadcast_to(ids_buf[slot][0:1], (rows, rows)).T
        allowed = other == own
        if slot == nsp:
            key_pos = lax.broadcasted_iota(jnp.int32, (rows, rows), 0)
            query_pos = lax.broadcasted_iota(jnp.int32, (rows, rows), 1)
            allowed = allowed & (key_pos <= query_pos)
        bias[slot * rows:(slot + 1) * rows, :] = jnp.where(allowed, 0.0, NEGATIVE)

    width = blocks * rows
    factor = scale * math.log2(math.e)

    def group_step(g, carry):
        load_q(g).wait()
        load_g(g).wait()
        for dist in range(1, nsp + 1):
            @pl.when(me - dist >= 0)
            def _():
                send_kv(g, dist).wait_recv()

        keys = kv_buf[g, :, 0].reshape(width, DH)
        values = kv_buf[g, :, 1].reshape(width, DH)
        keys_t = keys.T
        values_t = values.T
        for pair in range(heads // PAIR):
            first = pair * PAIR

            def stacked(buf):
                return jnp.concatenate(
                    [buf[g, :, (first + i) * DH:(first + i + 1) * DH] for i in range(PAIR)], axis=0)

            queries = stacked(q_buf)
            grads = stacked(g_buf)
            wide_bias = jnp.concatenate([bias[...]] * PAIR, axis=1)
            nt = (((1,), (1,)), ((), ()))
            scores = lax.dot_general(keys, queries, nt, preferred_element_type=jnp.float32) + wide_bias
            top = jnp.max(scores, axis=0, keepdims=True)
            expo = jnp.exp2((scores - top) * factor)
            probs = expo * (1.0 / jnp.sum(expo, axis=0, keepdims=True))
            weights = probs.astype(jnp.bfloat16)
            pt_buf[:, first * rows:(first + PAIR) * rows] = weights
            out_t = jnp.dot(values_t, weights, preferred_element_type=jnp.float32)
            dprobs = lax.dot_general(values, grads, nt, preferred_element_type=jnp.float32)
            delta = jnp.sum(probs * dprobs, axis=0, keepdims=True)
            dscores = (probs * (dprobs - delta)).astype(jnp.bfloat16)
            ds_buf[:, first * rows:(first + PAIR) * rows] = dscores
            grad_t = jnp.dot(keys_t, dscores, preferred_element_type=jnp.float32) * scale
            for i in range(PAIR):
                cols = slice((first + i) * DH, (first + i + 1) * DH)
                att_buf[g, :, cols] = out_t[:, i * rows:(i + 1) * rows].T.astype(jnp.bfloat16)
                gq_buf[g, :, cols] = grad_t[:, i * rows:(i + 1) * rows].T.astype(jnp.bfloat16)

        store_att(g).start()
        store_gq(g).start()
        all_q = jnp.concatenate([q_buf[g, :, h * DH:(h + 1) * DH] for h in range(heads)], axis=0)
        all_g = jnp.concatenate([g_buf[g, :, h * DH:(h + 1) * DH] for h in range(heads)], axis=0)
        for slot in range(blocks):
            part = slice(slot * rows, (slot + 1) * rows)
            grad_k = jnp.dot(ds_buf[part, :], all_q, preferred_element_type=jnp.float32) * scale
            grad_v = jnp.dot(pt_buf[part, :], all_g, preferred_element_type=jnp.float32)
            if slot == nsp:
                part_own[g, 0] = grad_k
                part_own[g, 1] = grad_v
            else:
                part_send[g, nsp - slot - 1, 0] = grad_k.astype(jnp.bfloat16)
                part_send[g, nsp - slot - 1, 1] = grad_v.astype(jnp.bfloat16)
        for dist in range(1, nsp + 1):
            @pl.when(me - dist >= 0)
            def _():
                send_part(g, dist).start()
        return carry

    lax.fori_loop(0, groups, group_step, 0)

    for dist in range(1, nsp + 1):
        @pl.when(me + dist >= total)
        def _():
            def clear(g, carry):
                part_recv[g, dist - 1] = jnp.zeros((2, rows, DH), jnp.bfloat16)
                return carry

            lax.fori_loop(0, groups, clear, 0)

    def finish(g, carry):
        for dist in range(1, nsp + 1):
            @pl.when(me + dist < total)
            def _():
                send_part(g, dist).wait_recv()

        acc = part_own[g]
        for dist in range(1, nsp + 1):
            acc = acc + part_recv[g, dist - 1].astype(jnp.float32)
        acc = acc.astype(jnp.bfloat16)
        gk_buf[g] = acc[0]
        gv_buf[g] = acc[1]
        pltpu.make_async_copy(gk_buf.at[g], gk_hbm.at[:, key_cols(g)], fin_sem.at[g, 0]).start()
        pltpu.make_async_copy(gv_buf.at[g], gv_hbm.at[:, key_cols(g)], fin_sem.at[g, 1]).start()
        return carry

    lax.fori_loop(0, groups, finish, 0)

    def drain(g, carry):
        store_att(g).wait()
        store_gq(g).wait()
        pltpu.make_async_copy(gk_buf.at[g], gk_hbm.at[:, key_cols(g)], fin_sem.at[g, 0]).wait()
        pltpu.make_async_copy(gv_buf.at[g], gv_hbm.at[:, key_cols(g)], fin_sem.at[g, 1]).wait()
        for dist in range(1, nsp + 1):
            @pl.when(me + dist < total)
            def _():
                send_kv(g, dist).wait_send()

            @pl.when(me - dist >= 0)
            def _():
                send_part(g, dist).wait_send()
        return carry

    lax.fori_loop(0, groups, drain, 0)
    for dist in range(1, nsp + 1):
        @pl.when(me + dist < total)
        def _():
            send_ids(dist).wait_send()


def shards(queries, key_rows, value_rows, grad_out, doc_ids):
    ndp, nsp = lax.axis_size("dp"), lax.axis_size("sp")
    rows = queries.shape[0]
    groups = key_rows.shape[1] // DH
    heads = queries.shape[1] // key_rows.shape[1]
    blocks = nsp + 1
    ids = jnp.broadcast_to(doc_ids.astype(jnp.float32)[None, :], (8, rows))
    bf16, f32 = jnp.bfloat16, jnp.float32
    hbm = pl.BlockSpec(memory_space=pl.ANY)
    dma = pltpu.SemaphoreType.DMA
    return pl.pallas_call(
        functools.partial(kernel, ndp, nsp, groups, heads),
        out_shape=(
            jax.ShapeDtypeStruct(queries.shape, bf16),
            jax.ShapeDtypeStruct(queries.shape, bf16),
            jax.ShapeDtypeStruct(key_rows.shape, bf16),
            jax.ShapeDtypeStruct(key_rows.shape, bf16),
        ),
        in_specs=[hbm] * 5,
        out_specs=(hbm,) * 4,
        scratch_shapes=[
            pltpu.VMEM((groups, rows, heads * DH), bf16),
            pltpu.VMEM((groups, rows, heads * DH), bf16),
            pltpu.VMEM((groups, rows, heads * DH), bf16),
            pltpu.VMEM((groups, rows, heads * DH), bf16),
            pltpu.VMEM((groups, blocks, 2, rows, DH), bf16),
            pltpu.VMEM((blocks, 8, rows), f32),
            pltpu.VMEM((blocks * rows, rows), f32),
            pltpu.VMEM((blocks * rows, heads * rows), bf16),
            pltpu.VMEM((blocks * rows, heads * rows), bf16),
            pltpu.VMEM((groups, 2, rows, DH), f32),
            pltpu.VMEM((groups, nsp, 2, rows, DH), bf16),
            pltpu.VMEM((groups, nsp, 2, rows, DH), bf16),
            pltpu.VMEM((groups, rows, DH), bf16),
            pltpu.VMEM((groups, rows, DH), bf16),
            dma((groups, 2)),
            dma((groups, 2)),
            dma((groups, 2)),
            dma((groups, nsp)),
            dma((groups, nsp)),
            dma((nsp,)),
            dma((nsp,)),
            dma,
            dma((groups, nsp)),
            dma((groups, nsp)),
            dma((groups, 2)),
        ],
        compiler_params=pltpu.CompilerParams(
            collective_id=0, has_side_effects=True, vmem_limit_bytes=60 * 1024 * 1024),
        name="attention",
    )(queries, key_rows, value_rows, grad_out, ids)


def solution(mesh):
    rows = P(("dp", "sp"), None)
    return jax.shard_map(
        shards,
        mesh=mesh,
        in_specs=(rows, rows, rows, rows, P(("dp", "sp"))),
        out_specs=(rows, rows, rows, rows),
        check_vma=False,
    )
```

time: 383 us -> 108 us (0.28)
  waiting for transfers between devices: 147 us -> 0 us
  matrix products: 135 us -> 0 us
  Pallas kernels: 0 us -> 99.5 us
  local copies, waits for them, and re-layouts: 47.4 us -> 6.58 us
  other arithmetic: 18.1 us -> 0.66 us
  between operations: 13.9 us -> 0.65 us
  blocking collectives: 10.2 us -> 0 us
  starting transfers between devices: 8.57 us -> 0 us
    pallas_call x0 -> x1, Pallas kernels: none -> 99.5 us  [shards(): pl.pallas_call(functools.partial(kernel, ndp, nsp, groups, heads), out_sh...]
    dot_general x40 -> x0, matrix products: 91.1 us -> none  [the longest x8 24.7 us: group_grads(): jnp.einsum('hqw,qhd->wd', weights, grad_group, preferred_element_type=jnp...]
    reduce_scatter x2 -> x0, waiting for transfers between devices: 70.1 us -> none  [the longest x1 43.3 us: shards(): lax.psum_scatter(key_acc[row_len:] + later_keys, 'sp', scatter_dimension=...]
    all_gather x2 -> x0, waiting for transfers between devices: 60 us -> none  [the longest x1 31.9 us: shards(): lax.all_gather(key_rows, 'sp', axis=0, tiled=True)]
    sub x16 -> x0, matrix products: 43.5 us -> none  [group_probs(): expo = jnp.exp(scores - jnp.max(scores, axis=-1, keepdims=True))]
    ppermute x5 -> x0, waiting for transfers between devices: 17.2 us -> none  [from_behind(): return lax.ppermute(block, axis, route)]
    dynamic_slice x25 -> x0, local copies, waits for them, and re-layouts: 10.8 us -> none  [the longest x24 10.7 us: advance(): lax.map(lambda items: group_attend(items, mask), (query_block, key_window...]
    unnamed x14 -> x10, local copies, waits for them, and re-layouts: 16.8 us -> 5.98 us
  transfers between devices with their start and end apart: 9 -> 0, of which waited for: 6 -> 0; matrix products, arithmetic and copies ran while one was open for 7% -> 0% of each run, Pallas kernels for 0% -> 0%
where the time goes in v1:
time: 108 us; the launch traced here: 107 us
  Pallas kernels  99.5 us (92%)
  local copies, waits for them, and re-layouts  6.58 us (6%)
    pallas_call x1, Pallas kernels, shards(): pl.pallas_call(functools.partial(kernel, ndp, nsp, groups, heads), out_sh...  99.5 us
    unnamed x10, local copies, waits for them, and re-layouts  5.98 us

profile of v1, /device:TPU:0, one launch (start us, length us, event | category | flops | bytes accessed | tf_op | source)
XLA Modules:
  0.0 107.4 jit_solution(5122584860346149888)
XLA Ops:
  0.6 0.7 convert_element_type.3
  1.3 0.6 broadcast_in_dim.2.ids_hbm
  1.9 99.5 %attention.1 = (bf16[128,8192]{1,0:T(8,128)(2,1)}, bf16[128,8192]{1,0:T(8,128)(2,1)}, bf16[128,1024]{1,0:T(8,128)(2,1)}, bf16[128,1024]{1,0:T(8,128)(2,1)}) custom-call(bf16[128,8192]{1,0:T(8,128)(2,1)} %q_hbm.1, bf16[128,1024]{1,0:T(8,128)(2,1)} %k_hbm.1, bf16[128,1024]{1,0:T(8,128)(2,1)} %v_hbm.1, bf16[128,8192]{1,0:T(8,128)(2,1)} %g_hbm.1, ...), custom_call_target="tpu_custom_call" | custom-call | tf_op jit(solution)/shard_map/attention/pallas_call | solution.py:265
  101.4 0.0 copy-start
  101.4 3.2 %copy.13 = bf16[128,8192]{1,0:T(8,128)(2,1)} copy(bf16[128,8192]{1,0:T(8,128)(2,1)} %get-tuple-element.8) | data formatting | bytes 4194304
  104.7 0.0 copy-done
  104.7 0.0 copy-start.2
  104.7 0.0 copy-start.1
  104.7 1.3 %copy.14 = bf16[128,8192]{1,0:T(8,128)(2,1)} copy(bf16[128,8192]{1,0:T(8,128)(2,1)S(1)} %copy-done) | data formatting | bytes 4194304
  106.0 0.0 copy-done.2
  106.0 0.7 copy.15
  106.7 0.0 copy-done.1
  106.7 0.7 copy.16
Async XLA Ops:
  101.4 3.3 %copy-start = (bf16[128,8192]{1,0:T(8,128)(2,1)S(1)}, bf16[128,8192]{1,0:T(8,128)(2,1)}, u32[]{:S(2)}) copy-start(bf16[128,8192]{1,0:T(8,128)(2,1)} %get-tuple-element.9) | copy-start | bytes 6291460
  104.7 1.3 %copy-start.2 = (bf16[128,1024]{1,0:T(8,128)(2,1)S(1)}, bf16[128,1024]{1,0:T(8,128)(2,1)}, u32[]{:S(2)}) copy-start(bf16[128,1024]{1,0:T(8,128)(2,1)} %get-tuple-element.10) | copy-start | bytes 786436
  104.7 2.0 %copy-start.1 = (bf16[128,1024]{1,0:T(8,128)(2,1)S(1)}, bf16[128,1024]{1,0:T(8,128)(2,1)}, u32[]{:S(2)}) copy-start(bf16[128,1024]{1,0:T(8,128)(2,1)} %get-tuple-element.11) | copy-start | bytes 786436

commit v2 on v1

--- a/solution.py
+++ b/solution.py
@@ -23,15 +23,11 @@
     load_sem, out_sem, kv_load, kv_send, kv_recv, ids_send, ids_recv, ids_load,
     pg_send, pg_recv, fin_sem,
 ):
-    me = lax.axis_index("dp") * nsp + lax.axis_index("sp")
-    total = ndp * nsp
+    row, col = lax.axis_index("dp"), lax.axis_index("sp")
     blocks = nsp + 1
     rows = q_hbm.shape[0]
     scale = DH ** (-0.5)
 
-    def device(index):
-        return (index // nsp, lax.rem(index, nsp))
-
     def head_cols(g):
         return pl.ds(pl.multiple_of(g * (heads * DH), heads * DH), heads * DH)
 
@@ -56,23 +52,129 @@
     def store_gq(g):
         return pltpu.make_async_copy(gq_buf.at[g], gq_hbm.at[:, head_cols(g)], out_sem.at[g, 1])
 
-    def send_kv(g, dist):
+    def remote(src, dst, send_sem, recv_sem, target):
         return pltpu.make_async_remote_copy(
-            src_ref=kv_buf.at[g, nsp], dst_ref=kv_buf.at[g, nsp - dist],
-            send_sem=kv_send.at[g, dist - 1], recv_sem=kv_recv.at[g, dist - 1],
-            device_id=device(me + dist), device_id_type=MESH)
-
-    def send_ids(dist):
-        return pltpu.make_async_remote_copy(
-            src_ref=ids_buf.at[nsp], dst_ref=ids_buf.at[nsp - dist],
-            send_sem=ids_send.at[dist - 1], recv_sem=ids_recv.at[dist - 1],
-            device_id=device(me + dist), device_id_type=MESH)
-
-    def send_part(g, dist):
-        return pltpu.make_async_remote_copy(
-            src_ref=part_send.at[g, dist - 1], dst_ref=part_recv.at[g, dist - 1],
-            send_sem=pg_send.at[g, dist - 1], recv_sem=pg_recv.at[g, dist - 1],
-            device_id=device(me - dist), device_id_type=MESH)
+            src_ref=src, dst_ref=dst, send_sem=send_sem, recv_sem=recv_sem,
+            device_id=target, device_id_type=MESH)
+
+    up, down, later, earlier = (row, col + 1), (row, col - 1), (row + 1, col), (row - 1, col)
+    has_up, has_down, has_later, has_earlier = col + 1 < nsp, col >= 1, row + 1 < ndp, row >= 1
+
+    def kv_up(g, dist):
+        return remote(kv_buf.at[g, nsp - dist], kv_buf.at[g, nsp - dist - 1],
+                      kv_send.at[g, dist], kv_recv.at[g, dist], up)
+
+    def kv_down(g, dist):
+        return remote(kv_buf.at[g, nsp - dist], kv_buf.at[g, nsp - dist + 1],
+                      kv_send.at[g, dist], kv_recv.at[g, dist - 2], down)
+
+    def kv_later(g):
+        return remote(kv_buf.at[g, nsp], kv_buf.at[g, 0],
+                      kv_send.at[g, nsp + 1], kv_recv.at[g, nsp - 1], later)
+
+    def arrived(g, dist):
+        return remote(kv_buf.at[g, nsp], kv_buf.at[g, nsp - dist],
+                      kv_send.at[g, 0], kv_recv.at[g, dist - 1], up)
+
+    def part_down(g, dist):
+        return remote(part_send.at[g, dist - 1], part_recv.at[g, dist - 1],
+                      pg_send.at[g, dist - 1], pg_recv.at[g, dist - 1], down)
+
+    def part_up(g, dist):
+        return remote(part_send.at[g, dist - 1], part_recv.at[g, dist + 1],
+                      pg_send.at[g, dist - 1], pg_recv.at[g, dist + 1], up)
+
+    def part_earlier(g):
+        return remote(part_send.at[g, nsp - 1], part_recv.at[g, nsp + 1],
+                      pg_send.at[g, nsp - 1], pg_recv.at[g, nsp + 1], earlier)
+
+    def part_sent(g, dist):
+        return remote(part_send.at[g, dist - 1], part_recv.at[g, 0],
+                      pg_send.at[g, dist - 1], pg_recv.at[g, 0], up)
+
+    def part_arrived(g, slot):
+        return remote(part_send.at[g, 0], part_recv.at[g, slot],
+                      pg_send.at[g, 0], pg_recv.at[g, slot], up)
+
+    def ids_to(dist, target):
+        return remote(ids_buf.at[nsp], ids_buf.at[nsp - dist],
+                      ids_send.at[dist - 1], ids_recv.at[dist - 1], target)
+
+    def ids_target(dist):
+        index = row * nsp + col + dist
+        return (index // nsp, lax.rem(index, nsp))
+
+    def ids_source(dist):
+        index = row * nsp + col - dist
+        return (index // nsp, lax.rem(index, nsp))
+
+    def sends_ids(dist):
+        return row * nsp + col + dist < ndp * nsp
+
+    def gets_ids(dist):
+        return row * nsp + col - dist >= 0
+
+    def own_out(g):
+        load_k(g).wait()
+        load_v(g).wait()
+
+        @pl.when(has_up)
+        def _():
+            kv_up(g, 0).start()
+
+        @pl.when(has_later)
+        def _():
+            kv_later(g).start()
+
+    def gather(g, stage):
+        @pl.when(col >= stage)
+        def _():
+            arrived(g, stage).wait_recv()
+
+            if stage < nsp:
+                @pl.when(has_up)
+                def _():
+                    kv_up(g, stage).start()
+
+        dist = nsp + 1 - stage
+
+        @pl.when(has_earlier & (col < dist))
+        def _():
+            arrived(g, dist).wait_recv()
+
+            if dist >= 2:
+                @pl.when(has_down)
+                def _():
+                    kv_down(g, dist).start()
+
+    def add_part(g, dist):
+        part_arrived(g, dist).wait_recv()
+        mine = part_send[g, dist - 1].astype(jnp.float32)
+        theirs = part_recv[g, dist].astype(jnp.float32)
+        part_send[g, dist - 1] = (mine + theirs).astype(jnp.bfloat16)
+
+    def scatter_down(g):
+        for dist in range(1, nsp):
+            @pl.when(col >= dist)
+            def _():
+                @pl.when(has_up)
+                def _():
+                    add_part(g, dist)
+
+                part_down(g, dist).start()
+
+    def scatter_up(g):
+        for dist in range(nsp, 0, -1):
+            @pl.when(has_earlier & (col < dist))
+            def _():
+                @pl.when(has_down)
+                def _():
+                    add_part(g, dist)
+
+                if dist == nsp:
+                    part_earlier(g).start()
+                else:
+                    part_up(g, dist).start()
 
     ids_copy = pltpu.make_async_copy(ids_hbm, ids_buf.at[nsp], ids_load)
     ids_copy.start()
@@ -85,36 +187,26 @@
 
     barrier = pltpu.get_barrier_semaphore()
     for dist in range(1, nsp + 1):
-        @pl.when(me + dist < total)
-        def _():
-            pl.semaphore_signal(barrier, inc=1, device_id=device(me + dist), device_id_type=MESH)
-
-        @pl.when(me - dist >= 0)
-        def _():
-            pl.semaphore_signal(barrier, inc=1, device_id=device(me - dist), device_id_type=MESH)
-
-    peers = jnp.minimum(nsp, total - 1 - me) + jnp.minimum(nsp, me)
+        @pl.when(sends_ids(dist))
+        def _():
+            pl.semaphore_signal(barrier, inc=1, device_id=ids_target(dist), device_id_type=MESH)
+
+        @pl.when(gets_ids(dist))
+        def _():
+            pl.semaphore_signal(barrier, inc=1, device_id=ids_source(dist), device_id_type=MESH)
+
+    place = row * nsp + col
+    peers = jnp.minimum(nsp, ndp * nsp - 1 - place) + jnp.minimum(nsp, place)
     pl.semaphore_wait(barrier, peers)
 
     ids_copy.wait()
     for dist in range(1, nsp + 1):
-        @pl.when(me + dist < total)
-        def _():
-            send_ids(dist).start()
-
-    def start_kv(g, carry):
-        load_k(g).wait()
-        load_v(g).wait()
-        for dist in range(1, nsp + 1):
-            @pl.when(me + dist < total)
-            def _():
-                send_kv(g, dist).start()
-        return carry
-
-    lax.fori_loop(0, groups, start_kv, 0)
+        @pl.when(sends_ids(dist))
+        def _():
+            ids_to(dist, ids_target(dist)).start()
 
     for dist in range(1, nsp + 1):
-        @pl.when(me - dist < 0)
+        @pl.when(jnp.logical_not(gets_ids(dist)))
         def _():
             ids_buf[nsp - dist] = jnp.full((8, rows), -1.0, jnp.float32)
 
@@ -124,9 +216,11 @@
 
             lax.fori_loop(0, groups, clear, 0)
 
-        @pl.when(me - dist >= 0)
-        def _():
-            send_ids(dist).wait_recv()
+    own_out(0)
+    for dist in range(1, nsp + 1):
+        @pl.when(gets_ids(dist))
+        def _():
+            ids_to(dist, up).wait_recv()
 
     own = jnp.broadcast_to(ids_buf[nsp][0:1], (rows, rows))
     for slot in range(blocks):
@@ -141,14 +235,9 @@
     width = blocks * rows
     factor = scale * math.log2(math.e)
 
-    def group_step(g, carry):
+    def compute(g):
         load_q(g).wait()
         load_g(g).wait()
-        for dist in range(1, nsp + 1):
-            @pl.when(me - dist >= 0)
-            def _():
-                send_kv(g, dist).wait_recv()
-
         keys = kv_buf[g, :, 0].reshape(width, DH)
         values = kv_buf[g, :, 1].reshape(width, DH)
         keys_t = keys.T
@@ -195,32 +284,57 @@
             else:
                 part_send[g, nsp - slot - 1, 0] = grad_k.astype(jnp.bfloat16)
                 part_send[g, nsp - slot - 1, 1] = grad_v.astype(jnp.bfloat16)
-        for dist in range(1, nsp + 1):
-            @pl.when(me - dist >= 0)
-            def _():
-                send_part(g, dist).start()
+
+    def step(g, carry):
+        @pl.when((g + nsp >= 1) & (g + nsp < groups))
+        def _():
+            own_out(g + nsp)
+
+        for stage in range(1, nsp + 1):
+            ahead = g + nsp - stage
+
+            @pl.when((ahead >= 0) & (ahead < groups))
+            def _():
+                gather(ahead, stage)
+
+        @pl.when((g >= 0) & (g < groups))
+        def _():
+            compute(g)
+
+        lower = g - (nsp - 1 - col)
+
+        @pl.when((lower >= 0) & (lower < groups))
+        def _():
+            scatter_down(lower)
+
+        upper = g - col
+
+        @pl.when((upper >= 0) & (upper < groups))
+        def _():
+            scatter_up(upper)
+
         return carry
 
-    lax.fori_loop(0, groups, group_step, 0)
-
-    for dist in range(1, nsp + 1):
-        @pl.when(me + dist >= total)
+    lax.fori_loop(1 - nsp, groups + nsp - 1, step, 0)
+
+    for have, slot in ((has_up, 0), (has_later, nsp + 1)):
+        @pl.when(jnp.logical_not(have))
         def _():
             def clear(g, carry):
-                part_recv[g, dist - 1] = jnp.zeros((2, rows, DH), jnp.bfloat16)
+                part_recv[g, slot] = jnp.zeros((2, rows, DH), jnp.bfloat16)
                 return carry
 
             lax.fori_loop(0, groups, clear, 0)
 
     def finish(g, carry):
-        for dist in range(1, nsp + 1):
-            @pl.when(me + dist < total)
-            def _():
-                send_part(g, dist).wait_recv()
+        for have, slot in ((has_up, 0), (has_later, nsp + 1)):
+            @pl.when(have)
+            def _():
+                part_arrived(g, slot).wait_recv()
 
         acc = part_own[g]
-        for dist in range(1, nsp + 1):
-            acc = acc + part_recv[g, dist - 1].astype(jnp.float32)
+        for slot in (0, nsp + 1):
+            acc = acc + part_recv[g, slot].astype(jnp.float32)
         acc = acc.astype(jnp.bfloat16)
         gk_buf[g] = acc[0]
         gv_buf[g] = acc[1]
@@ -235,21 +349,34 @@
         store_gq(g).wait()
         pltpu.make_async_copy(gk_buf.at[g], gk_hbm.at[:, key_cols(g)], fin_sem.at[g, 0]).wait()
         pltpu.make_async_copy(gv_buf.at[g], gv_hbm.at[:, key_cols(g)], fin_sem.at[g, 1]).wait()
+        @pl.when(has_up)
+        def _():
+            kv_up(g, 0).wait_send()
+
+        @pl.when(has_later)
+        def _():
+            kv_later(g).wait_send()
+
         for dist in range(1, nsp + 1):
-            @pl.when(me + dist < total)
-            def _():
-                send_kv(g, dist).wait_send()
-
-            @pl.when(me - dist >= 0)
-            def _():
-                send_part(g, dist).wait_send()
+            @pl.when((col >= dist) & has_up)
+            def _():
+                kv_up(g, min(dist, nsp - 1)).wait_send()
+
+            @pl.when(has_earlier & (col < dist) & has_down)
+            def _():
+                kv_down(g, max(dist, 2)).wait_send()
+
+            @pl.when((col >= dist) | has_earlier)
+            def _():
+                part_sent(g, dist).wait_send()
+
         return carry
 
     lax.fori_loop(0, groups, drain, 0)
     for dist in range(1, nsp + 1):
-        @pl.when(me + dist < total)
-        def _():
-            send_ids(dist).wait_send()
+        @pl.when(sends_ids(dist))
+        def _():
+            ids_to(dist, ids_target(dist)).wait_send()
 
 
 def shards(queries, key_rows, value_rows, grad_out, doc_ids):
@@ -284,19 +411,19 @@
             pltpu.VMEM((blocks * rows, heads * rows), bf16),
             pltpu.VMEM((groups, 2, rows, DH), f32),
             pltpu.VMEM((groups, nsp, 2, rows, DH), bf16),
-            pltpu.VMEM((groups, nsp, 2, rows, DH), bf16),
+            pltpu.VMEM((groups, nsp + 2, 2, rows, DH), bf16),
             pltpu.VMEM((groups, rows, DH), bf16),
             pltpu.VMEM((groups, rows, DH), bf16),
             dma((groups, 2)),
             dma((groups, 2)),
             dma((groups, 2)),
-            dma((groups, nsp)),
+            dma((groups, nsp + 2)),
             dma((groups, nsp)),
             dma((nsp,)),
             dma((nsp,)),
             dma,
             dma((groups, nsp)),
-            dma((groups, nsp)),
+            dma((groups, nsp + 2)),
             dma((groups, 2)),
         ],
         compiler_params=pltpu.CompilerParams(

time: 108 us -> 90.1 us (0.83)
  the two profiles are of different devices: /device:TPU:0 before, /device:TPU:27 now
where the time goes in v2:
time: 90.1 us; the launch traced here: 89.9 us
  Pallas kernels  82.1 us (91%)
  local copies, waits for them, and re-layouts  6.58 us (7%)
    pallas_call x1, Pallas kernels, shards(): pl.pallas_call(functools.partial(kernel, ndp, nsp, groups, heads), out_sh...  82.1 us
    unnamed x10, local copies, waits for them, and re-layouts  5.98 us

profile of v2, /device:TPU:27, one launch (start us, length us, event | category | flops | bytes accessed | tf_op | source)
XLA Modules:
  0.0 89.9 jit_solution(16451202931360072877)
XLA Ops:
  0.6 0.7 convert_element_type.3
  1.3 0.6 broadcast_in_dim.2.ids_hbm
  1.9 82.1 %attention.1 = (bf16[128,8192]{1,0:T(8,128)(2,1)}, bf16[128,8192]{1,0:T(8,128)(2,1)}, bf16[128,1024]{1,0:T(8,128)(2,1)}, bf16[128,1024]{1,0:T(8,128)(2,1)}) custom-call(bf16[128,8192]{1,0:T(8,128)(2,1)} %q_hbm.1, bf16[128,1024]{1,0:T(8,128)(2,1)} %k_hbm.1, bf16[128,1024]{1,0:T(8,128)(2,1)} %v_hbm.1, bf16[128,8192]{1,0:T(8,128)(2,1)} %g_hbm.1, ...), custom_call_target="tpu_custom_call" | custom-call | tf_op jit(solution)/shard_map/attention/pallas_call | solution.py:392
  84.0 0.0 copy-start
  84.0 3.2 %copy.13 = bf16[128,8192]{1,0:T(8,128)(2,1)} copy(bf16[128,8192]{1,0:T(8,128)(2,1)} %get-tuple-element.8) | data formatting | bytes 4194304
  87.2 0.0 copy-done
  87.2 0.0 copy-start.2
  87.2 0.0 copy-start.1
  87.2 1.3 %copy.14 = bf16[128,8192]{1,0:T(8,128)(2,1)} copy(bf16[128,8192]{1,0:T(8,128)(2,1)S(1)} %copy-done) | data formatting | bytes 4194304
  88.5 0.0 copy-done.2
  88.5 0.7 copy.15
  89.2 0.0 copy-done.1
  89.2 0.7 copy.16
Async XLA Ops:
  84.0 3.3 %copy-start = (bf16[128,8192]{1,0:T(8,128)(2,1)S(1)}, bf16[128,8192]{1,0:T(8,128)(2,1)}, u32[]{:S(2)}) copy-start(bf16[128,8192]{1,0:T(8,128)(2,1)} %get-tuple-element.9) | copy-start | bytes 6291460
  87.2 1.3 %copy-start.2 = (bf16[128,1024]{1,0:T(8,128)(2,1)S(1)}, bf16[128,1024]{1,0:T(8,128)(2,1)}, u32[]{:S(2)}) copy-start(bf16[128,1024]{1,0:T(8,128)(2,1)} %get-tuple-element.10) | copy-start | bytes 786436
  87.2 2.0 %copy-start.1 = (bf16[128,1024]{1,0:T(8,128)(2,1)S(1)}, bf16[128,1024]{1,0:T(8,128)(2,1)}, u32[]{:S(2)}) copy-start(bf16[128,1024]{1,0:T(8,128)(2,1)} %get-tuple-element.11) | copy-start | bytes 786436
